TPU v7x, 256 devices: a whole 4x4x8 slice. The times are simulated.
256 devices in a mesh: rep: 1, dp: 256 (over x, y, z, core).
Axes of the slice: x: 4, y: 4, z: 8, core: 2. Of those that a mesh axis runs over, the one named last changes fastest.
Arguments:
- x: bfloat16 [256, 1024, 1024], P(('rep', 'dp'))
- dy: bfloat16 [256, 1024, 1024], P(('rep', 'dp'))
- w_gate: bfloat16 [2, 1024, 2560], replicated
- w_up: bfloat16 [2, 1024, 2560], replicated
- w_down: bfloat16 [2, 2560, 1024], replicated
- m_w_gate: float32 [2, 1024, 2560], P(None, 'dp')
- m_w_up: float32 [2, 1024, 2560], P(None, 'dp')
- m_w_down: float32 [2, 2560, 1024], P(None, 'dp')
- v_w_gate: float32 [2, 1024, 2560], P(None, 'dp')
- v_w_up: float32 [2, 1024, 2560], P(None, 'dp')
- v_w_down: float32 [2, 2560, 1024], P(None, 'dp')
Outputs:
- output 1: bfloat16 [2, 1024, 2560], P('rep')
- output 2: bfloat16 [2, 1024, 2560], P('rep')
- output 3: bfloat16 [2, 2560, 1024], P('rep')
- output 4: float32 [2, 1024, 2560], P('rep', 'dp')
- output 5: float32 [2, 1024, 2560], P('rep', 'dp')
- output 6: float32 [2, 2560, 1024], P('rep', 'dp')
- output 7: float32 [2, 1024, 2560], P('rep', 'dp')
- output 8: float32 [2, 1024, 2560], P('rep', 'dp')
- output 9: float32 [2, 2560, 1024], P('rep', 'dp')
All inputs are finite; a program needn't handle non-finite values.
Results may differ from a plain program's by a relative error of at most 0.022.
Values are sent between devices in bfloat16 or wider.
A program may use at most 768 MiB of HBM per device.

v0:
```python
import jax
import jax.numpy as jnp
from jax import lax

NAMES = ("w_gate", "w_up", "w_down")


def matmul(a, w):
    return jnp.dot(a, w, preferred_element_type=jnp.float32).astype(jnp.bfloat16)


def normed(h):
    wide = h.astype(jnp.float32)
    scale = lax.rsqrt(jnp.mean(wide**2, -1, keepdims=True) + 1e-6)
    return (wide * scale).astype(jnp.bfloat16)


def layer(h, w):
    a = normed(h)
    gate = jnp.dot(a, w["w_gate"], preferred_element_type=jnp.float32)
    up = jnp.dot(a, w["w_up"], preferred_element_type=jnp.float32)
    return h + matmul((jax.nn.silu(gate) * up).astype(jnp.bfloat16), w["w_down"])


def adamw(w, m, v, g):
    m = 0.9 * m + 0.1 * g
    v = 0.95 * v + 0.05 * g * g
    step = m * lax.rsqrt(v + 1e-8) + 0.1 * w
    return (w - 0.02 * step).astype(jnp.bfloat16), m, v


def stack(weights, h):
    for number in range(weights["w_gate"].shape[0]):
        h = layer(h, {name: w[number] for name, w in weights.items()})
    return h


def solution(mesh):
    groups = mesh.shape["rep"]

    def step(x, dy, *arrays):
        weights, m, v = (arrays[i : i + 3] for i in (0, 3, 6))
        x, dy = (t.reshape(groups, -1, *t.shape[1:]) for t in (x, dy))

        def of_a_group(x, dy):
            _, back = jax.vjp(lambda w: stack(w, x), dict(zip(NAMES, weights, strict=True)))
            by_weights = back(dy)[0]
            gradients = [by_weights[name].astype(jnp.float32) for name in NAMES]
            new = [adamw(w.astype(jnp.float32), m, v, g) for w, m, v, g in zip(weights, m, v, gradients, strict=True)]
            return tuple(one[which] for which in range(3) for one in new)

        return tuple(t.reshape(-1, *t.shape[2:]) for t in jax.vmap(of_a_group)(x, dy))

    return step
```

profile of v0, /device:TPU:1, one launch (start us, length us, event | category | flops | bytes accessed | tf_op | source)
XLA Modules:
  0.0 1048.0 jit_solution(13821638368388086925)
XLA Ops:
  7.2 0.0 copy-start.2
  7.2 0.0 all-gather.14.cloned.1.call-start
  7.2 2.2 fusion.59
  9.4 3.9 copy.6
  13.4 0.0 copy-done.2
  13.4 7.6 fusion.46
  21.0 0.0 copy-start
  21.1 9.6 fusion.44
  30.7 0.0 copy-done
  30.7 0.0 copy-start.1
  30.7 0.0 copy-start.9
  30.7 3.5 fusion.26
  34.2 0.7 copy-done.1
  34.9 0.0 copy-done.9
  34.9 9.6 fusion.63
  44.6 0.0 slice-start.3
  44.6 0.0 slice-start.4
  44.6 11.5 %fusion.36 = f32[1024,2560]{1,0:T(8,128)} fusion(bf16[2,1024,2560]{2,1,0:T(8,128)(2,1)} %param, bf16[1,1024,1024]{1,2,0:T(8,128)(2,1)S(1)} %get-tuple-element.34, f32[1024]{0:T(1024)S(1)} %bitcast.326), kind=kOutput, calls=%fused_computation.53 | convolution fusion | flops 5371854848 | bytes 17829888 | tf_op jit(solution)/vmap(jvp())/dot_general | solution.py:20
  56.2 0.0 copy-done.5
  56.2 11.2 %fusion.39 = f32[1024,2560]{1,0:T(8,128)} fusion(bf16[2,1024,2560]{2,1,0:T(8,128)(2,1)} %param.5, bf16[1,1024,1024]{1,2,0:T(8,128)(2,1)S(1)} %get-tuple-element.34, f32[1024]{0:T(1024)S(1)} %bitcast.327), kind=kOutput, calls=%fused_computation.56 | convolution fusion | flops 5371854848 | bytes 17829888 | tf_op jit(solution)/vmap(jvp())/dot_general | solution.py:21
  67.4 7.5 convolution_convert_fusion.1
  74.9 2.9 copy.7
  77.7 11.8 %fusion.24 = bf16[1024,1024]{0,1:T(8,128)(2,1)} fusion(bf16[1024,2560]{1,0:T(8,128)(2,1)} %convolution_convert_fusion.1, f32[1024,2560]{1,0:T(8,128)} %fusion.36, bf16[2,1024,2560]{2,1,0:T(8,128)(2,1)} %param.5), kind=kOutput, calls=%fused_computation.38 | convolution fusion | flops 5384437760 | bytes 23068672 | tf_op jit(solution)/vmap(transpose(jvp()))/dot_general | solution.py:21
  89.5 16.5 %fusion.65 = (f32[1024]{0:T(1024)S(1)}, bf16[1024,1024]{0,1:T(8,128)(2,1)}) fusion(bf16[1,1024,1024]{1,2,0:T(8,128)(2,1)} %copy-done.5, bf16[1024,1024]{0,1:T(8,128)(2,1)} %fusion.24, bf16[2,1024,2560]{2,1,0:T(8,128)(2,1)} %param, f32[1024,2560]{1,0:T(8,128)} %fusion.36, f32[1024,2560]{1,0:T(8,128)} %fusion.39, bf16[1024,2560]{1,0:T(8,128)(2,1)} %convolution_convert_fusion.1), kind=kOutput, calls=%fused_computation.82 | convolution fusion | flops 5403835392 | bytes 37752832 | tf_op jit(solution)/vmap(transpose(jvp()))/dot_general | solution.py:20
  106.1 3.8 fusion.68
  109.8 0.0 slice-start
  109.8 0.0 slice-start.1
  109.9 10.9 %fusion.125 = f32[1024,2560]{0,1:T(8,128)} fusion(bf16[1024,1024]{0,1:T(8,128)(2,1)S(1)} %fusion.68, bf16[1024,2560]{1,0:T(8,128)(2,1)} %copy-done.4), kind=kOutput, calls=%fused_computation.156 | convolution fusion | flops 5368709120 | bytes 17825792 | tf_op jit(solution)/vmap(transpose(jvp()))/dot_general | solution.py:9
  120.8 10.0 convolution_convert_fusion
  130.8 10.7 %fusion.2 = f32[2560,1024]{0,1:T(8,128)} fusion(bf16[1024,2560]{1,0:T(8,128)(2,1)} %convolution_convert_fusion, f32[1024,2560]{1,0:T(8,128)S(1)} %bitcast.319, bf16[1,1024,1024]{2,1,0:T(8,128)(2,1)S(1)} %copy-done.3, f32[1024]{0:T(1024)S(1)} %add_rsqrt_fusion), kind=kOutput, calls=%fused_computation.8 | convolution fusion | flops 5387583488 | bytes 28315648 | tf_op jit(solution)/vmap(transpose(jvp()))/dot_general | solution.py:21
  141.5 14.9 %fusion.10 = f32[2560,1024]{0,1:T(8,128)} fusion(f32[1024,2560]{1,0:T(8,128)} %copy-done, f32[1024,2560]{1,0:T(8,128)} %copy-done.1, bf16[1024,2560]{1,0:T(8,128)(2,1)} %convolution_convert_fusion, bf16[1,1024,1024]{2,1,0:T(8,128)(2,1)S(1)} %copy-done.3, f32[1024]{0:T(1024)S(1)} %add_rsqrt_fusion), kind=kOutput, calls=%fused_computation.15 | convolution fusion | flops 5400690688 | bytes 38801408 | tf_op jit(solution)/vmap(transpose(jvp()))/dot_general | solution.py:20
  156.4 0.0 copy-done.6
  156.4 14.2 %fusion.77 = f32[2560,1024]{0,1:T(8,128)} fusion(bf16[1,1024,1024]{1,2,0:T(8,128)(2,1)S(1)} %copy-done.6, f32[1024]{0:T(1024)S(1)} %bitcast.329, f32[1024,2560]{1,0:T(8,128)} %fusion.36, f32[1024,2560]{1,0:T(8,128)} %fusion.39, bf16[1024,2560]{1,0:T(8,128)(2,1)} %convolution_convert_fusion.1), kind=kOutput, calls=%fused_computation.91 | convolution fusion | flops 5400690688 | bytes 38801408 | tf_op jit(solution)/vmap(transpose(jvp()))/dot_general | solution.py:20
  170.6 12.0 %fusion.22 = f32[2560,1024]{0,1:T(8,128)} fusion(bf16[1024,2560]{1,0:T(8,128)(2,1)} %convolution_convert_fusion.1, f32[1024,2560]{1,0:T(8,128)} %fusion.36, bf16[1,1024,1024]{1,2,0:T(8,128)(2,1)S(1)} %copy-done.6, f32[1024]{0:T(1024)S(1)} %bitcast.330), kind=kOutput, calls=%fused_computation.37 | convolution fusion | flops 5387583488 | bytes 28315648 | tf_op jit(solution)/vmap(transpose(jvp()))/dot_general | solution.py:21
  182.6 12.8 %fusion.28 = f32[2560,1024]{1,0:T(8,128)} fusion(f32[1024,2560]{1,0:T(8,128)} %fusion.39, f32[1024,2560]{1,0:T(8,128)} %fusion.36, bf16[1,1024,1024]{2,1,0:T(8,128)(2,1)S(1)} %copy-done.8), kind=kOutput, calls=%fused_computation.46 | convolution fusion | flops 5384437760 | bytes 33554432 | tf_op jit(solution)/vmap(transpose(jvp()))/dot_general | solution.py:9
  195.4 0.0 copy-start.11
  195.4 0.0 copy-start.12
  195.4 0.0 copy-start.13
  195.4 476.1 %all-reduce.14 = (bf16[2560,1024]{0,1:T(8,128)(2,1)}, bf16[2560,1024]{0,1:T(8,128)(2,1)}, bf16[2560,1024]{0,1:T(8,128)(2,1)}, bf16[2560,1024]{0,1:T(8,128)(2,1)}...) all-reduce(f32[2560,1024]{0,1:T(8,128)} %fusion.10, ...), channel_id=14, replica_groups=mesh['axis_0'=256] {'axis_0'}, use_global_device_ids=true, to_apply=%add.1.clone.clone | all-reduce | flops 15728640 | bytes 94371840
  671.5 0.8 fusion.104
  672.3 0.8 fusion.105
  673.2 0.0 copy-done.14
  673.2 0.0 copy-done.15
  673.2 1.0 fusion.89
  674.2 0.7 copy.12
  674.9 0.0 all-gather.14.cloned.1.call-update
  674.9 0.0 all-gather.12.cloned.1.call-start
  674.9 0.8 fusion.112
  675.8 1.7 fusion.108
  677.5 0.6 copy.9
  678.1 0.0 all-gather.12.cloned.1.call-update
  678.1 0.3 all-gather.10.cloned.1.call-start
  678.4 0.8 fusion.110
  679.3 1.7 fusion.109
  680.9 0.6 copy.8
  681.6 0.0 all-gather.10.cloned.1.call-update
  681.6 0.7 copy.16
  682.3 0.7 copy.17
  683.0 107.6 %all-gather.14.cloned.1.call-done = bf16[1,2,2560,1024]{3,1,0,2:T(2,128)(2,1)} async-done(((bf16[1,2,10,1024]{3,1,0,2:T(2,128)(2,1)}), bf16[1,2,2560,1024]{3,1,0,2:T(2,128)(2,1)}) %all-gather.14.cloned.1.call-update) | async-done | bytes 10485776 | tf_op jit(solution)/reshape | solution.py:52
  790.6 11.4 %copy.15 = bf16[2,2560,1024]{2,1,0:T(8,128)(2,1)} copy(bf16[2,2560,1024]{2,0,1:T(2,128)(2,1)} %bitcast.320) | data formatting | bytes 20971520
  802.0 109.0 %all-gather.12.cloned.1.call-done = bf16[1,2,1024,2560]{3,1,0,2:T(2,128)(2,1)} async-done(((bf16[1,2,4,2560]{3,1,0,2:T(2,128)(2,1)}), bf16[1,2,1024,2560]{3,1,0,2:T(2,128)(2,1)}) %all-gather.12.cloned.1.call-update) | async-done | bytes 10485776 | tf_op jit(solution)/reshape | solution.py:52
  911.0 9.7 copy.14
  920.7 110.7 %all-gather.10.cloned.1.call-done = bf16[1,2,1024,2560]{3,1,0,2:T(2,128)(2,1)} async-done(((bf16[1,2,4,2560]{3,1,0,2:T(2,128)(2,1)}), bf16[1,2,1024,2560]{3,1,0,2:T(2,128)(2,1)}) %all-gather.10.cloned.1.call-update) | async-done | bytes 10485776 | tf_op jit(solution)/reshape | solution.py:52
  1031.4 9.7 copy.13
  (31 shorter events, 0.1 us)
Async XLA Ops:
  7.2 6.2 copy-start.2
  7.2 783.4 %all-gather.14.cloned.1.call-start = ((), (), s32[]{:S(2)}) async-start(), calls=%async_computation.2 | async-start | bytes 10526720 | tf_op jit(solution)/reshape | solution.py:52
  21.0 9.6 copy-start
  30.7 4.2 copy-start.1
  30.7 4.2 copy-start.9
  34.9 9.6 copy-start.4
  44.6 11.6 %copy-start.5 = (bf16[1,1024,1024]{1,2,0:T(8,128)(2,1)}, bf16[1,1024,1024]{1,2,0:T(8,128)(2,1)S(1)}, u32[]{:S(2)}) copy-start(bf16[1,1024,1024]{1,2,0:T(8,128)(2,1)S(1)} %get-tuple-element.34) | copy-start | bytes 6291460
  44.6 22.7 %slice-start.3 = ((s8[10485760]{0:T(1024)(128)(4,1)}), s8[4194304]{0:T(1024)(128)(4,1)S(1)}, s32[]{:S(2)}) async-start(s8[10485760]{0:T(1024)(128)(4,1)} %bitcast.332), calls=%async_computation.6 | async-start | bytes 8388608
  44.6 22.7 %slice-start.4 = ((s8[10485760]{0:T(1024)(128)(4,1)}), s8[4194304]{0:T(1024)(128)(4,1)S(1)}, s32[]{:S(2)}) async-start(s8[10485760]{0:T(1024)(128)(4,1)} %bitcast.332), calls=%async_computation.7 | async-start | bytes 8388608
  56.2 11.2 %copy-start.7 = (bf16[1,1024,1024]{2,1,0:T(8,128)(2,1)S(1)}, bf16[1,1024,1024]{2,1,0:T(8,128)(2,1)}, u32[]{:S(2)}) copy-start(bf16[1,1024,1024]{2,1,0:T(8,128)(2,1)} %param.2) | copy-start | bytes 6291460
  56.2 11.2 %slice-start.5 = ((s8[10485760]{0:T(1024)(128)(4,1)}), s8[2097152]{0:T(1024)(128)(4,1)S(1)}, s32[]{:S(2)}) async-start(s8[10485760]{0:T(1024)(128)(4,1)} %bitcast.332), calls=%async_computation.8 | async-start | bytes 4194304
  109.8 21.0 %slice-start = ((s8[10485760]{0:T(1024)(128)(4,1)}), s8[4194304]{0:T(1024)(128)(4,1)S(1)}, s32[]{:S(2)}) async-start(s8[10485760]{0:T(1024)(128)(4,1)} %bitcast.318), calls=%async_computation.3 | async-start | bytes 8388608
  109.8 20.9 %slice-start.1 = ((s8[10485760]{0:T(1024)(128)(4,1)}), s8[4194304]{0:T(1024)(128)(4,1)S(1)}, s32[]{:S(2)}) async-start(s8[10485760]{0:T(1024)(128)(4,1)} %bitcast.318), calls=%async_computation.4 | async-start | bytes 8388608
  120.8 10.0 slice-start.2
  120.8 10.0 copy-start.3
  141.5 14.9 %copy-start.6 = (bf16[1,1024,1024]{1,2,0:T(8,128)(2,1)S(1)}, bf16[1,1024,1024]{1,2,0:T(8,128)(2,1)}, u32[]{:S(2)}) copy-start(bf16[1,1024,1024]{1,2,0:T(8,128)(2,1)} %copy-done.5) | copy-start | bytes 6291460
  170.6 12.0 %copy-start.8 = (bf16[1,1024,1024]{2,1,0:T(8,128)(2,1)S(1)}, bf16[1,1024,1024]{2,1,0:T(8,128)(2,1)}, u32[]{:S(2)}) copy-start(bf16[1,1024,1024]{2,1,0:T(8,128)(2,1)} %param.2) | copy-start | bytes 6291460
  195.3 477.8 %copy-start.14 = (f32[2,10,1024]{2,0,1:T(2,128)S(1)}, f32[2,10,1024]{2,0,1:T(2,128)}, u32[]{:S(2)}) copy-start(f32[2,10,1024]{2,0,1:T(2,128)} %param.10) | copy-start | bytes 245764
  195.3 477.8 %copy-start.15 = (f32[2,10,1024]{2,0,1:T(2,128)S(1)}, f32[2,10,1024]{2,0,1:T(2,128)}, u32[]{:S(2)}) copy-start(f32[2,10,1024]{2,0,1:T(2,128)} %param.9) | copy-start | bytes 245764
  195.3 480.4 %copy-start.10 = (f32[2,4,2560]{2,1,0:T(4,128)S(1)}, f32[2,4,2560]{2,1,0:T(4,128)}, u32[]{:S(2)}) copy-start(f32[2,4,2560]{2,1,0:T(4,128)} %param.8) | copy-start | bytes 245764
  195.4 480.4 %copy-start.11 = (f32[2,4,2560]{2,1,0:T(4,128)S(1)}, f32[2,4,2560]{2,1,0:T(4,128)}, u32[]{:S(2)}) copy-start(f32[2,4,2560]{2,1,0:T(4,128)} %param.7) | copy-start | bytes 245764
  195.4 483.9 %copy-start.12 = (f32[2,4,2560]{2,1,0:T(4,128)S(1)}, f32[2,4,2560]{2,1,0:T(4,128)}, u32[]{:S(2)}) copy-start(f32[2,4,2560]{2,1,0:T(4,128)} %param.6) | copy-start | bytes 245764
  195.4 483.9 %copy-start.13 = (f32[2,4,2560]{2,1,0:T(4,128)S(1)}, f32[2,4,2560]{2,1,0:T(4,128)}, u32[]{:S(2)}) copy-start(f32[2,4,2560]{2,1,0:T(4,128)} %param.1) | copy-start | bytes 245764
  674.9 236.1 %all-gather.12.cloned.1.call-start = ((), (), s32[]{:S(2)}) async-start(), calls=%async_computation.1 | async-start | bytes 10526720 | tf_op jit(solution)/reshape | solution.py:52
  678.1 353.2 %all-gather.10.cloned.1.call-start = ((), (), s32[]{:S(2)}) async-start(), calls=%async_computation | async-start | bytes 10526720 | tf_op jit(solution)/reshape | solution.py:52
Sparse Core Ops, SparseCore 0:
  675.0 115.5 all-gather.13
  795.0 115.9 all-gather.11
  915.4 115.9 all-gather.9
where the time goes:
time: 1060 us; the launch traced here: 1050 us
  blocking collectives  476 us (45%)
  waiting for transfers between devices  327 us (31%)
  matrix products  171 us (16%)
  local copies, waits for them, and re-layouts  45.1 us (4%)
  between operations  14.5 us (1%)
  other arithmetic  13.9 us (1%)
    unnamed x1, blocking collectives  476 us
    reshape x3, waiting for transfers between devices, step(): t.reshape(-1, *t.shape[2:])  327 us
    dot_general x5, matrix products, layer(): gate = jnp.dot(a, w['w_gate'], preferred_element_type=jnp.float32)  64.7 us
    dot_general x5, matrix products, layer(): up = jnp.dot(a, w['w_up'], preferred_element_type=jnp.float32)  55.3 us
    dot_general x5, matrix products, matmul(): jnp.dot(a, w, preferred_element_type=jnp.float32).astype(jnp.bfloat16)  50.8 us
    unnamed x51, local copies, waits for them, and re-layouts  39.8 us
  transfers between devices with their start and end apart: 3, of which 3 were waited for; matrix products, arithmetic and copies ran while one was open for 3% of the time, Pallas kernels for 0%

commit v1 on v0

v1 whole, which is shorter than its diff:
```python
import functools

import jax
import jax.numpy as jnp
from jax import lax
from jax.experimental import pallas as pl
from jax.experimental.pallas import tpu as pltpu
from jax.sharding import PartitionSpec as P

NAMES = ("w_gate", "w_up", "w_down")
MESH = pl.DeviceIdType.MESH
F32, BF16 = jnp.float32, jnp.bfloat16
SIZES = {"x": 4, "y": 4, "z": 8}
VMEM_LIMIT = 64 * 1024 * 1024 - 64 * 1024


RING, DIRECT = "ring", "direct"
COLOURS = (
    (("x", RING), ("y", RING), ("z", DIRECT)),
    (("y", RING), ("x", RING), ("z", DIRECT)),
    (("z", RING), ("x", DIRECT), ("y", DIRECT)),
)
WIDE, TALL = "wide", "tall"
PART = {WIDE: ((0, 384), (384, 384), (768, 512)), TALL: ((0, 16), (16, 16), (32, 8))}
HALF = {WIDE: 1280, TALL: 512}
ROWS = {WIDE: 8, TALL: 40}
ORDER = ((TALL, 1), (WIDE, 1), (WIDE, 3), (TALL, 0), (WIDE, 0), (WIDE, 2))


class Me:
    def __init__(self):
        index = lax.axis_index("dp")
        self.core = lax.rem(index, 2)
        chip = index // 2
        self.at = {
            "z": lax.rem(chip, SIZES["z"]),
            "y": lax.rem(chip // SIZES["z"], SIZES["y"]),
            "x": chip // (SIZES["z"] * SIZES["y"]),
        }
        self.sign = 1 - 2 * self.core

    def off(self, d, by):
        return lax.rem(self.at[d] + by + SIZES[d], SIZES[d])

    def device(self, core=None, **at):
        at = {**self.at, **at}
        core = self.core if core is None else core
        return (0, ((at["x"] * SIZES["y"] + at["y"]) * SIZES["z"] + at["z"]) * 2 + core)

    def barrier(self):
        sem = pltpu.get_barrier_semaphore()

        def signal(peer):
            pl.semaphore_signal(sem, inc=1, device_id=peer, device_id_type=MESH)

        for d, n in SIZES.items():
            each(n - 1, lambda i, d=d: signal(self.device(**{d: self.off(d, i + 1)})))
        signal(self.device(core=1 - self.core))
        signal(self.device(core=1 - self.core, z=self.pair()))
        pl.semaphore_wait(sem, sum(SIZES.values()) - 1)

    def pair(self):
        return self.at["z"] + 1 - 2 * lax.rem(self.at["z"], 2)


def dims(kind, free):
    return tuple(SIZES[d] // (2 if kind == TALL and d == "z" else 1) for d in free)


def view(ref, kind, free, fixed, colour=None, base=0, own=False):
    index = [(fixed[d] // 2 if kind == TALL and d == "z" else fixed[d]) if d in fixed else slice(None) for d in free]
    if own and not (kind == TALL and "z" in free and "z" in fixed):
        return ref.at[(*index, slice(None), slice(None))]
    if kind == WIDE:
        first, size = (0, HALF[WIDE]) if colour is None else PART[WIDE][colour]
        rows, columns = slice(None), pl.ds(_at(base, first), size)
    else:
        rows = slice(None) if own or colour is None else pl.ds(*PART[TALL][colour])
        if "z" in free and "z" in fixed:
            columns = pl.ds(pl.multiple_of(base + lax.rem(fixed["z"], 2) * 256, 256), 256)
        else:
            columns = pl.ds(_at(base, 0), HALF[TALL])
    return ref.at[(*index, rows, columns)]


def _at(base, first):
    return first if isinstance(base, int) and base == 0 else pl.multiple_of(base + first, 128)


def block(kind, colour, free):
    first, size = PART[kind][colour]
    tail = (8, size) if kind == WIDE else (size, HALF[TALL] if "z" in free else HALF[TALL] // 2)
    return dims(kind, free) + tail


def lengths(n):
    return n // 2, (n - 1) // 2


def reduce_buffers(kind):
    shapes = {}
    for c, phases in enumerate(COLOURS):
        free = ["x", "y", "z"]
        for p, (d, how) in enumerate(phases):
            free.remove(d)
            shape = block(kind, c, tuple(free))
            count = SIZES[d] - 1
            shapes[c, p] = (count, *shape)
    return shapes


class Copies:
    def __init__(self, send, recv):
        self.send, self.recv, self.all, self.used = send, recv, {}, 0

    def start(self, key, src, dst, to):
        self.start_all(key, 1, lambda i: (src, dst, to))

    def start_all(self, key, count, make):
        first = self.used
        self.used += count

        def copy(i):
            src, dst, to = make(i)
            return pltpu.make_async_remote_copy(
                src_ref=src, dst_ref=dst, send_sem=self.send.at[first + i], recv_sem=self.recv.at[first + i], device_id=to, device_id_type=MESH
            )

        self.all[key] = count, copy
        each(count, lambda i: copy(i).start())

    def arrived(self, key):
        count, copy = self.all[key]
        each(count, lambda i: copy(i).wait_recv())

    def sent(self):
        for count, copy in self.all.values():
            each(count, lambda i, copy=copy: copy(i).wait_send())


def each(count, do):
    if count == 1:
        do(0)
    else:

        @pl.loop(0, count)
        def _(i):
            do(i)


def total(parts):
    return functools.reduce(jnp.add, [p[...].astype(F32) for p in parts])


def reduce_colour(me, copies, key, kind, colour, grads, received, last):
    free, fixed = ("x", "y", "z"), {}
    parts = [lambda at, r=r: view(r, kind, ("x", "y", "z"), at, colour) for r in grads]
    out = parts[0]

    def add(at, more):
        rest = [d for d in free if d not in at]
        if len(rest) >= 2:
            first = rest[0]

            @pl.loop(0, SIZES[first])
            def _(i):
                now = {**at, first: i}
                out(now)[...] = total([p(now) for p in parts + more]).astype(BF16)
        else:
            out(at)[...] = total([p(at) for p in parts + more]).astype(BF16)

    for phase, (d, how) in enumerate(COLOURS[colour]):
        n, buffer = SIZES[d], received(colour, phase)
        left = tuple(e for e in ("x", "y", "z") if e not in fixed and e != d)

        def slot(i, buffer=buffer, left=left):
            return lambda at: view(buffer.at[i], kind, left, {e: v for e, v in at.items() if e in left}, colour, own=True)

        if how == RING:
            long, short = lengths(n)
            ways = ((me.sign, long, 0, "l"), (-me.sign, short, long, "s"))
            for s in range(long):
                for sign, length, base, name in ways:
                    if s >= length:
                        continue
                    to = me.off(d, sign * (length - s))
                    at = {**fixed, d: to}
                    if s:
                        copies.arrived((key, colour, phase, name, s - 1))
                    add(at, [slot(base + s - 1)] if s else [])
                    copies.start(
                        (key, colour, phase, name, s), out(at), buffer.at[base + s], me.device(**{d: me.off(d, sign)})
                    )
                yield
            for sign, length, base, name in ways:
                if length:
                    copies.arrived((key, colour, phase, name, length - 1))
            parts = parts + [slot(base + length - 1) for sign, length, base, name in ways if length]
        else:

            def make(i, d=d, fixed=fixed, buffer=buffer, add=add, out=out):
                to = me.off(d, i + 1)
                return out({**fixed, d: to}), buffer.at[i], me.device(**{d: to})

            each(n - 1, lambda i: add({**fixed, d: me.off(d, i + 1)}, []))
            copies.start_all((key, colour, phase), n - 1, make)
            yield
            copies.arrived((key, colour, phase))
            parts = parts + [slot(i) for i in range(n - 1)]
        fixed = {**fixed, d: me.at[d]}
    last(colour, total([p(fixed) for p in parts]).astype(BF16).astype(F32))


def reduce_kernel(*refs):
    ins, outs, rest = refs[:6], refs[6:8], list(refs[8:])
    own = {WIDE: rest[0], TALL: rest[1]}
    other = {WIDE: rest[2], TALL: rest[3]}
    sums = {WIDE: rest[4], TALL: rest[5]}
    cross = {WIDE: rest[6], TALL: rest[7]}
    shares = rest[8]
    load, send, recv = rest[9:12]
    bufs = {}
    for kind in (WIDE, TALL):
        for k in reduce_buffers(kind):
            bufs[kind, k] = rest[12 + len(bufs)]
    me = Me()
    me.barrier()
    copies = Copies(send, recv)
    loads = []
    for i, (kind, j) in enumerate(ORDER):
        half = HALF[kind]
        src = ins[i].at[..., pl.ds(pl.multiple_of(me.core * half, 256), half)]
        copy = pltpu.make_async_copy(src, own[kind].at[j], load.at[i])
        copy.start()
        loads.append(copy)
        src = ins[i].at[..., pl.ds(pl.multiple_of((1 - me.core) * half, 256), half)]
        copies.start((i, "half"), src, other[kind].at[j], me.device(core=1 - me.core))

    def colours(i):
        kind, j = ORDER[i]
        loads[i].wait()
        copies.arrived((i, "half"))

        def last(colour, value):
            first, size = PART[kind][colour]
            if kind == WIDE:
                sums[WIDE][j, 0, :, first : first + size] = value[:4]
                sums[WIDE][j, 1, :, first : first + size] = value[4:]
            else:
                sums[TALL][j, first : first + size, :] = value

        gens = [
            reduce_colour(me, copies, i, kind, c, (own[kind].at[j], other[kind].at[j]), lambda c, p: bufs[kind, (c, p)].at[j], last)
            for c in range(3)
        ]
        while gens:
            gens = [g for g in gens if next(g, 0) is None]
            yield
        if kind == WIDE:
            copies.start((i, "rows"), sums[WIDE].at[j, 1 - me.core], cross[WIDE].at[j], me.device(core=1 - me.core))
        else:
            for q in range(4):
                shares[j, q] = sums[TALL][j, 10 * q : 10 * q + 10, :]
            b = lax.rem(me.at["z"], 2)
            mine = 2 * b + me.core
            for o, (z, core) in enumerate(((me.at["z"], 1 - me.core), (me.pair(), me.core), (me.pair(), 1 - me.core))):
                q = 2 * lax.rem(z, 2) + core
                copies.start((i, "rows", o), shares.at[j, q], cross[TALL].at[j, mine], me.device(core=core, z=z))
        yield
        if kind == WIDE:
            copies.arrived((i, "rows"))
            outs[0][j, me.core] = sums[WIDE][j, me.core]
            outs[0][j, 1 - me.core] = cross[WIDE][j]
        else:
            for o in range(3):
                copies.arrived((i, "rows", o))
            for q in range(4):
                outs[1][j, q] = jnp.where(q == mine, shares[j, q], cross[TALL][j, q])

    run([colours(i) for i in range(6)], 3)
    copies.sent()


def run(gens, apart):
    steps = [(i * apart, i, g) for i, g in enumerate(gens)]
    t = 0
    live = set(range(len(gens)))
    while live:
        for start, i, g in steps:
            if i in live and t >= start and next(g, 0) == 0:
                live.discard(i)
        t += 1


def full_shape(kind):
    return dims(kind, ("x", "y", "z")) + (ROWS[kind], HALF[kind])


def reduce_scatter(grads):
    scratch = [
        pltpu.VMEM((4, *full_shape(WIDE)), BF16),
        pltpu.VMEM((2, *full_shape(TALL)), BF16),
        pltpu.VMEM((4, *full_shape(WIDE)), BF16),
        pltpu.VMEM((2, *full_shape(TALL)), BF16),
        pltpu.VMEM((4, 2, 4, 1280), F32),
        pltpu.VMEM((2, 40, 256), F32),
        pltpu.VMEM((4, 4, 1280), F32),
        pltpu.VMEM((2, 4, 10, 256), F32),
        pltpu.VMEM((2, 4, 10, 256), F32),
        pltpu.SemaphoreType.DMA((6,)),
        pltpu.SemaphoreType.DMA((256,)),
        pltpu.SemaphoreType.DMA((256,)),
    ]
    for kind, many in ((WIDE, 4), (TALL, 2)):
        scratch += [pltpu.VMEM((many, *shape), BF16) for shape in reduce_buffers(kind).values()]
    return pl.pallas_call(
        reduce_kernel,
        out_shape=(jax.ShapeDtypeStruct((4, 2, 4, 1280), F32), jax.ShapeDtypeStruct((2, 4, 10, 256), F32)),
        in_specs=[pl.BlockSpec(memory_space=pl.ANY)] * 6,
        out_specs=(pl.BlockSpec(memory_space=pltpu.VMEM), pl.BlockSpec(memory_space=pltpu.VMEM)),
        scratch_shapes=scratch,
        compiler_params=pltpu.CompilerParams(collective_id=0, has_side_effects=True, vmem_limit_bytes=VMEM_LIMIT),
        name="reduce_scatter",
    )(*grads)


def gather_colour(me, copies, key, kind, colour, ref):
    base = me.core * HALF[kind]
    fixed = dict(me.at)

    def part(at):
        return view(ref, kind, ("x", "y", "z"), at, colour, base)

    phases = COLOURS[colour][::-1]
    for phase, (d, how) in enumerate(phases):
        n, lastly = SIZES[d], phase == len(phases) - 1
        rest = {e: v for e, v in fixed.items() if e != d}
        here = part(fixed)

        def across(name, at):
            if lastly:
                copies.start((key, colour, "across", name), part(at), part(at), me.device(core=1 - me.core))

        if how == RING:
            long, short = lengths(n)
            ways = ((me.sign, long, "l"), (-me.sign, short, "s"))
            for s in range(long):
                for sign, length, name in ways:
                    if s >= length:
                        continue
                    at = {**rest, d: me.off(d, -sign * s)}
                    if s:
                        copies.arrived((key, colour, phase, name, s - 1))
                    copies.start((key, colour, phase, name, s), part(at), part(at), me.device(**{d: me.off(d, sign)}))
                    if s:
                        across((name, s - 1), at)
                if s == 0:
                    across("own", fixed)
                yield
            for sign, length, name in ways:
                if length:
                    copies.arrived((key, colour, phase, name, length - 1))
                    across((name, length - 1), {**rest, d: me.off(d, -sign * length)})
        else:
            copies.start_all(
                (key, colour, phase), n - 1, lambda i, d=d, here=here: (here, here, me.device(**{d: me.off(d, i + 1)}))
            )
            yield
            copies.arrived((key, colour, phase))
        fixed = rest
    yield
    names = ["own"]
    d, how = phases[-1]
    long, short = lengths(SIZES[d])
    names += [("l", s) for s in range(long)] + [("s", s) for s in range(short)]
    for name in names:
        copies.arrived((key, colour, "across", name))


def gather_kernel(*refs):
    wide, tall, outs, rest = refs[0], refs[1], refs[2:8], refs[8:]
    cross = {WIDE: rest[0], TALL: rest[1]}
    stage = {WIDE: rest[2], TALL: rest[3]}
    forty, put, send, recv = rest[4:8]
    me = Me()
    me.barrier()
    copies = Copies(send, recv)
    mine = 2 * lax.rem(me.at["z"], 2) + me.core

    for i, (kind, j) in enumerate(ORDER):
        if kind == WIDE:
            copies.start((i, "rows"), wide.at[j, 1 - me.core], cross[WIDE].at[j], me.device(core=1 - me.core))
        else:
            for o, (z, core) in enumerate(((me.at["z"], 1 - me.core), (me.pair(), me.core), (me.pair(), 1 - me.core))):
                q = 2 * lax.rem(z, 2) + core
                copies.start((i, "rows", o), tall.at[j, q], cross[TALL].at[j, mine], me.device(core=core, z=z))

    def colours(i):
        kind, j = ORDER[i]
        if kind == WIDE:
            copies.arrived((i, "rows"))
            own, theirs = wide[j, me.core], cross[WIDE][j]
            first = me.core == 0
            rows = [jnp.where(first, own, theirs), jnp.where(first, theirs, own)]
            stage[WIDE][j] = jnp.concatenate(rows, axis=0).astype(BF16)
        else:
            for o in range(3):
                copies.arrived((i, "rows", o))
            for q in range(4):
                forty[10 * q : 10 * q + 10, :] = jnp.where(q == mine, tall[j, q], cross[TALL][j, q])
            stage[TALL][j] = forty[...].astype(BF16)
        copy = pltpu.make_async_copy(
            stage[kind].at[j], view(outs[i], kind, ("x", "y", "z"), me.at, None, me.core * HALF[kind]), put.at[i]
        )
        copy.start()
        copy.wait()
        gens = [gather_colour(me, copies, i, kind, c, outs[i]) for c in range(3)]
        while gens:
            gens = [g for g in gens if next(g, 0) is None]
            yield

    run([colours(i) for i in range(6)], 3)
    copies.sent()


def all_gather(wide, tall):
    scratch = [
        pltpu.VMEM((4, 4, 1280), F32),
        pltpu.VMEM((2, 4, 10, 256), F32),
        pltpu.VMEM((4, 8, 1280), BF16),
        pltpu.VMEM((2, 40, 256), BF16),
        pltpu.VMEM((40, 256), F32),
        pltpu.SemaphoreType.DMA((6,)),
        pltpu.SemaphoreType.DMA((384,)),
        pltpu.SemaphoreType.DMA((384,)),
    ]
    return pl.pallas_call(
        gather_kernel,
        out_shape=tuple(
            jax.ShapeDtypeStruct((*dims(kind, ("x", "y", "z")), ROWS[kind], 2 * HALF[kind]), BF16) for kind, _ in ORDER
        ),
        in_specs=[pl.BlockSpec(memory_space=pltpu.VMEM)] * 2,
        out_specs=(pl.BlockSpec(memory_space=pl.ANY),) * 6,
        scratch_shapes=scratch,
        compiler_params=pltpu.CompilerParams(collective_id=1, has_side_effects=True),
        name="all_gather",
    )(wide, tall)


def matmul(a, w):
    return jnp.dot(a, w, preferred_element_type=F32).astype(BF16)


def normed(h):
    wide = h.astype(F32)
    scale = lax.rsqrt(jnp.mean(wide**2, -1, keepdims=True) + 1e-6)
    return (wide * scale).astype(BF16)


def layer(h, w):
    a = normed(h)
    gate = jnp.dot(a, w["w_gate"], preferred_element_type=F32)
    up = jnp.dot(a, w["w_up"], preferred_element_type=F32)
    return h + matmul((jax.nn.silu(gate) * up).astype(BF16), w["w_down"])


def adamw(w, m, v, g):
    m = 0.9 * m + 0.1 * g
    v = 0.95 * v + 0.05 * g * g
    step = m * lax.rsqrt(v + 1e-8) + 0.1 * w
    return (w - 0.02 * step).astype(BF16), m, v


def stack(weights, h):
    for w in weights:
        h = layer(h, w)
    return h


def split(g, kind):
    return g.reshape(*dims(kind, ("x", "y", "z")), ROWS[kind], 2 * HALF[kind])


def reduced(grads):
    ordered = []
    for kind, j in ORDER:
        name = "w_down" if kind == TALL else NAMES[j // 2]
        ordered.append(split(grads[j % 2][name], kind))
    wide, tall = reduce_scatter(ordered)
    wide = wide.transpose(0, 2, 1, 3).reshape(2, 2, 4, 2560)
    tall = tall.reshape(2, 2, 2, 10, 256).transpose(0, 3, 2, 1, 4).reshape(2, 10, 1024)
    return wide[0], wide[1], tall


def gathered(gate, up, down):
    wide = jnp.stack([gate, up]).reshape(4, 4, 2, 1280).transpose(0, 2, 1, 3).astype(F32)
    tall = down.reshape(2, 10, 2, 2, 256).transpose(0, 3, 2, 1, 4).reshape(2, 4, 10, 256).astype(F32)
    new = all_gather(wide, tall)
    by = {key: w.reshape(-1, w.shape[-1]) for key, w in zip(ORDER, new, strict=True)}
    return (
        jnp.stack([by[WIDE, 0], by[WIDE, 1]]),
        jnp.stack([by[WIDE, 2], by[WIDE, 3]]),
        jnp.stack([by[TALL, 0], by[TALL, 1]]),
    )


def solution(mesh):
    def step(x, dy, *arrays):
        weights, m, v = (arrays[i : i + 3] for i in (0, 3, 6))
        layers = [{name: w[l] for name, w in zip(NAMES, weights, strict=True)} for l in range(2)]
        _, back = jax.vjp(lambda w: stack(w, x[0]), layers)
        gradients = reduced(back(dy[0])[0])
        index = lax.axis_index("dp")
        news = []
        for w, mm, vv, g in zip(weights, m, v, gradients, strict=True):
            rows = mm.shape[1]
            mine = lax.dynamic_slice_in_dim(w, index * rows, rows, 1)
            news.append(adamw(mine.astype(F32), mm, vv, g))
        new = gathered(*(n[0] for n in news))
        return (*new, *(n[1] for n in news), *(n[2] for n in news))

    batch, whole, rows = P(("rep", "dp")), P(), P(None, "dp")
    return jax.shard_map(
        step,
        mesh=mesh,
        in_specs=(batch, batch, *(whole,) * 3, *(rows,) * 6),
        out_specs=(*(P("rep"),) * 3, *(P("rep", "dp"),) * 6),
        check_vma=False,
    )
```

time: 1060 us -> 482 us (0.45)
  blocking collectives: 476 us -> 0 us
  waiting for transfers between devices: 327 us -> 0 us
  Pallas kernels: 0 us -> 269 us
  local copies, waits for them, and re-layouts: 45.1 us -> 9.51 us
  other arithmetic: 13.9 us -> 36.4 us
  between operations: 14.5 us -> 1.39 us
  matrix products: 171 us -> 158 us
    unnamed x1 -> x0, blocking collectives: 476 us -> none
    reshape x3 -> x0, waiting for transfers between devices: 327 us -> none  [step(): t.reshape(-1, *t.shape[2:])]
    pallas_call x0 -> x2, Pallas kernels: none -> 269 us  [the longest x1 138 us: reduce_scatter(): pl.pallas_call(reduce_kernel, out_shape=(jax.ShapeDtypeStruct((4, 2, 4, 1...]
    unnamed x51 -> x36, local copies, waits for them, and re-layouts: 39.8 us -> 5.81 us
    another operation x0 -> x5, other arithmetic: none -> 29.4 us  [the longest x1 9.17 us: gathered(): jnp.stack([by[WIDE, 2], by[WIDE, 3]])]
    dot_general x15, matrix products: 171 us -> 158 us  [the longest x5 57.4 us: layer(): gate = jnp.dot(a, w['w_gate'], preferred_element_type=F32)]
  transfers between devices with their start and end apart: 3 -> 0, of which waited for: 3 -> 0; matrix products, arithmetic and copies ran while one was open for 3% -> 0% of each run, Pallas kernels for 0% -> 0%
where the time goes in v1:
time: 482 us; the launch traced here: 474 us
  Pallas kernels  269 us (56%)
  matrix products  158 us (33%)
  other arithmetic  36.4 us (8%)
  local copies, waits for them, and re-layouts  9.51 us (2%)
    pallas_call x1, Pallas kernels, reduce_scatter(): pl.pallas_call(reduce_kernel, out_shape=(jax.ShapeDtypeStruct((4, 2, 4, 1...  138 us
    pallas_call x1, Pallas kernels, all_gather(): pl.pallas_call(gather_kernel, out_shape=tuple((jax.ShapeDtypeStruct((*dim...  130 us
    dot_general x5, matrix products, layer(): gate = jnp.dot(a, w['w_gate'], preferred_element_type=F32)  57.4 us
    dot_general x5, matrix products, layer(): up = jnp.dot(a, w['w_up'], preferred_element_type=F32)  55.8 us
    dot_general x5, matrix products, matmul(): return jnp.dot(a, w, preferred_element_type=F32).astype(BF16)  45 us

profile of v1, /device:TPU:1, one launch (start us, length us, event | category | flops | bytes accessed | tf_op | source)
XLA Modules:
  0.0 473.9 jit_solution(5002718039046767741)
XLA Ops:
  0.6 2.9 copy.20
  3.5 0.0 copy-start
  3.5 0.0 slice-start.6
  3.5 0.5 fusion.43
  4.0 0.0 copy-start.3
  4.0 0.0 slice-start.7
  4.1 0.0 slice-start.8
  4.1 11.7 %fusion.31 = f32[1024,2560]{1,0:T(8,128)} fusion(bf16[2,1024,2560]{2,1,0:T(8,128)(2,1)} %param.13, bf16[1,1024,1024]{2,1,0:T(8,128)(2,1)} %param.11, f32[1024]{0:T(1024)S(1)} %add_rsqrt_fusion), kind=kOutput, calls=%fused_computation.53 | convolution fusion | flops 5371854848 | bytes 17829888 | tf_op jit(solution)/shard_map/jvp()/dot_general | solution.py:462
  15.7 0.0 copy-done.5
  15.7 0.0 slice-done.6
  15.7 0.0 copy-done.3
  15.7 0.0 slice-done.7
  15.7 0.0 slice-done.8
  15.8 12.2 %multiply_convert_fusion.1 = (bf16[1024,2560]{1,0:T(8,128)(2,1)}, f32[1024,2560]{1,0:T(8,128)}) fusion(f32[1024,2560]{1,0:T(8,128)} %fusion.31, bf16[2,1024,2560]{2,1,0:T(8,128)(2,1)S(1)} %bitcast.118, bf16[1,1024,1024]{2,1,0:T(8,128)(2,1)S(1)} %copy-done.3, f32[1024]{0:T(1024)S(1)} %add_rsqrt_fusion), kind=kOutput, calls=%fused_computation.20 | convolution fusion | flops 5387583488 | bytes 33558528 | tf_op jit(solution)/shard_map/jvp()/dot_general | solution.py:463
  28.0 0.0 copy-done
  28.0 9.5 %fusion.47 = (f32[1024]{0:T(1024)S(1)}, bf16[1024,1024]{0,1:T(8,128)(2,1)S(1)}) fusion(bf16[1024,2560]{1,0:T(8,128)(2,1)} %get-tuple-element.36, bf16[2,2560,1024]{2,1,0:T(8,128)(2,1)} %param.15, bf16[1,1024,1024]{1,2,0:T(8,128)(2,1)S(1)} %copy.20), kind=kOutput, calls=%fused_computation.69 | convolution fusion | flops 5373950976 | bytes 14684160 | tf_op jit(solution)/shard_map/jvp()/dot_general | solution.py:451
  37.5 0.0 copy-start.2
  37.5 0.0 slice-start.2
  37.5 0.0 copy-start.4
  37.5 11.5 %fusion.20 = f32[1024,2560]{1,0:T(8,128)} fusion(bf16[2,1024,2560]{2,1,0:T(8,128)(2,1)} %param.14, bf16[1024,1024]{0,1:T(8,128)(2,1)S(1)} %get-tuple-element.39, f32[1024]{0:T(1024)S(1)} %fusion.82), kind=kOutput, calls=%fused_computation.42 | convolution fusion | flops 5371854848 | bytes 17829888 | tf_op jit(solution)/shard_map/jvp()/dot_general | solution.py:463
  49.1 0.0 slice-done
  49.1 0.0 slice-done.1
  49.1 0.0 slice-done.2
  49.1 0.0 copy-done.4
  49.1 7.6 %convolution_convert_fusion.3 = bf16[1024,2560]{1,0:T(8,128)(2,1)} fusion(bf16[2,2560,1024]{2,1,0:T(8,128)(2,1)S(1)} %bitcast.114, bf16[1,1024,1024]{2,1,0:T(8,128)(2,1)S(1)} %copy-done.4), kind=kOutput, calls=%fused_computation.35 | convolution fusion | flops 5371330560 | bytes 12582912 | tf_op jit(solution)/shard_map/transpose(jvp())/dot_general | solution.py:451
  56.7 16.4 %fusion.2 = (bf16[1024,2560]{1,0:T(8,128)(2,1)S(1)}, f32[1024,2560]{1,0:T(8,128)}) fusion(f32[1024,2560]{1,0:T(8,128)} %fusion.20, bf16[1024,2560]{1,0:T(8,128)(2,1)} %convolution_convert_fusion.3, bf16[2,1024,2560]{2,1,0:T(8,128)(2,1)} %param.13, bf16[1024,1024]{0,1:T(8,128)(2,1)S(1)} %get-tuple-element.39, f32[1024]{0:T(1024)S(1)} %fusion.82), kind=kOutput, calls=%fused_computation.8 | convolution fusion | flops 5403312128 | bytes 38801408 | tf_op jit(solution)/shard_map/jvp()/dot_general | solution.py:462
  73.2 11.7 %convolution_convert_fusion.4 = bf16[2560,1024]{1,0:T(8,128)(2,1)} fusion(f32[1024,2560]{1,0:T(8,128)} %fusion.20, bf16[1,1024,1024]{2,1,0:T(8,128)(2,1)S(1)} %copy-done.4, f32[1024,2560]{1,0:T(8,128)} %get-tuple-element.41), kind=kOutput, calls=%fused_computation.36 | convolution fusion | flops 5387059200 | bytes 28311552 | tf_op jit(solution)/shard_map/transpose(jvp())/dot_general | solution.py:451
  84.8 7.3 %convolution_convert_fusion = bf16[1024,2560]{1,0:T(8,128)(2,1)} fusion(bf16[1024,2560]{1,0:T(8,128)(2,1)S(1)} %get-tuple-element.40, bf16[1024,1024]{0,1:T(8,128)(2,1)S(1)} %get-tuple-element.39, f32[1024]{0:T(1024)S(1)} %fusion.82), kind=kOutput, calls=%fused_computation.29 | convolution fusion | flops 5371854848 | bytes 12587008 | tf_op jit(solution)/shard_map/transpose(jvp())/dot_general | solution.py:462
  92.1 0.0 copy-done.7
  92.1 10.7 %fusion.13 = bf16[1024,2560]{1,0:T(8,128)(2,1)} fusion(bf16[1024,2560]{1,0:T(8,128)(2,1)S(1)} %copy-done.7, bf16[1024,1024]{0,1:T(8,128)(2,1)S(1)} %get-tuple-element.39, f32[1024]{0:T(1024)S(1)} %fusion.82, f32[1024,2560]{1,0:T(8,128)} %get-tuple-element.41), kind=kOutput, calls=%fused_computation.30 | convolution fusion | flops 5390204928 | bytes 23072768 | tf_op jit(solution)/shard_map/transpose(jvp())/dot_general | solution.py:463
  102.8 10.8 %fusion.11 = bf16[1024,1024]{0,1:T(8,128)(2,1)S(1)} fusion(bf16[1024,2560]{1,0:T(8,128)(2,1)} %convolution_convert_fusion.3, bf16[2,1024,2560]{2,1,0:T(8,128)(2,1)} %param.14, f32[1024,2560]{1,0:T(8,128)} %get-tuple-element.41), kind=kOutput, calls=%fused_computation.27 | convolution fusion | flops 5384437760 | bytes 23068672 | tf_op jit(solution)/shard_map/transpose(jvp())/dot_general | solution.py:463
  113.6 0.0 copy-done.2
  113.6 9.6 %fusion.49 = (f32[1024]{0:T(1024)S(1)}, bf16[1024,1024]{0,1:T(8,128)(2,1)}) fusion(bf16[1024,1024]{0,1:T(8,128)(2,1)S(1)} %get-tuple-element.39, bf16[1024,1024]{0,1:T(8,128)(2,1)S(1)} %fusion.11, bf16[1024,2560]{1,0:T(8,128)(2,1)S(1)} %get-tuple-element.40, bf16[2,1024,2560]{2,1,0:T(8,128)(2,1)} %param.13), kind=kOutput, calls=%fused_computation.71 | convolution fusion | flops 5373950976 | bytes 16781312 | tf_op jit(solution)/shard_map/transpose(jvp())/dot_general | solution.py:462
  123.2 2.9 copy.21
  126.1 0.0 slice-start.3
  126.1 3.9 fusion.51
  130.0 0.0 slice-start.4
  130.0 0.0 slice-start.5
  130.0 10.3 %convolution_convert_fusion.2 = bf16[2560,1024]{1,0:T(8,128)(2,1)} fusion(bf16[1024,2560]{1,0:T(8,128)(2,1)} %get-tuple-element.36, bf16[1024,1024]{0,1:T(8,128)(2,1)S(1)} %fusion.51), kind=kOutput, calls=%fused_computation.34 | convolution fusion | flops 5371330560 | bytes 12582912 | tf_op jit(solution)/shard_map/transpose(jvp())/dot_general | solution.py:451
  140.3 0.0 slice-done.3
  140.3 0.0 slice-done.4
  140.3 0.0 slice-done.5
  140.4 0.0 copy-start.1
  140.4 0.0 copy-start.6
  140.4 5.9 %convolution_convert_fusion.1 = bf16[1024,2560]{1,0:T(8,128)(2,1)S(1)} fusion(bf16[1024,1024]{0,1:T(8,128)(2,1)S(1)} %fusion.51, bf16[2,2560,1024]{2,1,0:T(8,128)(2,1)S(1)} %bitcast.116), kind=kOutput, calls=%fused_computation.33 | convolution fusion | flops 5371330560 | bytes 12582912 | tf_op jit(solution)/shard_map/transpose(jvp())/dot_general | solution.py:451
  146.3 0.0 copy-done.1
  146.3 0.0 copy-done.6
  146.3 12.5 %fusion.14 = bf16[1024,2560]{1,0:T(8,128)(2,1)} fusion(f32[1024,2560]{1,0:T(8,128)} %fusion.31, f32[1024,2560]{1,0:T(8,128)} %get-tuple-element.37, bf16[1024,2560]{1,0:T(8,128)(2,1)S(1)} %convolution_convert_fusion.1, bf16[1,1024,1024]{1,2,0:T(8,128)(2,1)S(1)} %copy-done.1, f32[1024]{0:T(1024)S(1)} %copy-done.6), kind=kOutput, calls=%fused_computation.31 | convolution fusion | flops 5403312128 | bytes 33558528 | tf_op jit(solution)/shard_map/transpose(jvp())/dot_general | solution.py:462
  158.8 10.5 %fusion.17 = bf16[1024,2560]{1,0:T(8,128)(2,1)} fusion(bf16[1024,2560]{1,0:T(8,128)(2,1)S(1)} %convolution_convert_fusion.1, bf16[1,1024,1024]{1,2,0:T(8,128)(2,1)S(1)} %copy-done.1, f32[1024]{0:T(1024)S(1)} %copy-done.6, f32[1024,2560]{1,0:T(8,128)} %fusion.31), kind=kOutput, calls=%fused_computation.32 | convolution fusion | flops 5390204928 | bytes 23072768 | tf_op jit(solution)/shard_map/transpose(jvp())/dot_general | solution.py:463
  169.3 138.2 %reduce_scatter.1 = (f32[4,2,4,1280]{3,2,1,0:T(4,128)}, f32[2,4,10,256]{3,2,1,0:T(8,128)}) custom-call(bf16[4,4,4,40,1024]{4,3,2,1,0:T(8,128)(2,1)} %bitcast.101, bf16[4,4,8,8,2560]{4,3,2,1,0:T(8,128)(2,1)} %bitcast.102, bf16[4,4,8,8,2560]{4,3,2,1,0:T(8,128)(2,1)} %bitcast.103, bf16[4,4,4,40,1024]{4,3,2,1,0:T(8,128)(2,1)} %bitcast.104, ...), custom_call_target="tpu_custom_call" | custom-call | tf_op jit(solution)/shard_map/reduce_scatter/pallas_call | solution.py:316
  307.5 0.9 fusion.91
  308.4 2.0 fusion.79
  310.4 0.1 pad_maximum_fusion.3
  310.5 0.7 convert_bitcast_fusion.refs_0_
  311.2 0.9 constant_dynamic-slice_fusion
  312.1 1.0 copy.23
  313.1 0.1 reshape.103
  313.2 1.8 fusion.81
  315.0 0.1 reshape.106
  315.1 0.7 copy.24
  315.7 130.3 %all_gather.1 = (bf16[4,4,4,40,1024]{4,3,2,1,0:T(8,128)(2,1)}, bf16[4,4,8,8,2560]{4,3,2,1,0:T(8,128)(2,1)}, bf16[4,4,8,8,2560]{4,3,2,1,0:T(8,128)(2,1)}, bf16[4,...) custom-call(f32[4,2,4,1280]{3,2,1,0:T(4,128)} %convert_bitcast_fusion.refs_0_, ...), custom_call_target="tpu_custom_call" | custom-call | tf_op jit(solution)/shard_map/all_gather/pallas_call | solution.py:437
  446.1 9.1 %pad_maximum_fusion = bf16[2,1024,2560]{2,1,0:T(8,128)(2,1)} fusion(bf16[1,1024,2560]{2,1,0:T(8,128)(2,1)} %bitcast.99, bf16[1,1024,2560]{2,1,0:T(8,128)(2,1)} %bitcast.100), kind=kLoop, calls=%fused_computation.12 | loop fusion | flops 5242880 | bytes 20971520 | tf_op jit(solution)/shard_map/stack | solution.py:501
  455.2 9.2 %pad_maximum_fusion.1 = bf16[2,1024,2560]{2,1,0:T(8,128)(2,1)} fusion(bf16[1,1024,2560]{2,1,0:T(8,128)(2,1)} %bitcast.97, bf16[1,1024,2560]{2,1,0:T(8,128)(2,1)} %bitcast.98), kind=kLoop, calls=%fused_computation.13 | loop fusion | flops 5242880 | bytes 20971520 | tf_op jit(solution)/shard_map/stack | solution.py:502
  464.4 9.1 %pad_maximum_fusion.2 = bf16[2,2560,1024]{2,1,0:T(8,128)(2,1)} fusion(bf16[1,2560,1024]{2,1,0:T(8,128)(2,1)} %bitcast.95, bf16[1,2560,1024]{2,1,0:T(8,128)(2,1)} %bitcast.96), kind=kLoop, calls=%fused_computation.14 | loop fusion | flops 5242880 | bytes 20971520 | tf_op jit(solution)/shard_map/stack | solution.py:503
  (10 shorter events, 0.0 us)
Async XLA Ops:
  3.5 24.5 %copy-start = (bf16[1,1024,1024]{1,2,0:T(8,128)(2,1)}, bf16[1,1024,1024]{1,2,0:T(8,128)(2,1)S(1)}, u32[]{:S(2)}) copy-start(bf16[1,1024,1024]{1,2,0:T(8,128)(2,1)S(1)} %copy.20) | copy-start | bytes 6291460
  3.5 12.2 %slice-start.6 = ((s8[10485760]{0:T(1024)(128)(4,1)}), s8[4194304]{0:T(1024)(128)(4,1)S(1)}, s32[]{:S(2)}) async-start(s8[10485760]{0:T(1024)(128)(4,1)} %bitcast.117), calls=%async_computation.6 | async-start | bytes 8388608
  4.0 11.7 %copy-start.5 = (f32[1024]{0:T(1024)}, f32[1024]{0:T(1024)S(1)}, u32[]{:S(2)}) copy-start(f32[1024]{0:T(1024)S(1)} %add_rsqrt_fusion) | copy-start | bytes 12292
  4.0 11.7 %copy-start.3 = (bf16[1,1024,1024]{2,1,0:T(8,128)(2,1)S(1)}, bf16[1,1024,1024]{2,1,0:T(8,128)(2,1)}, u32[]{:S(2)}) copy-start(bf16[1,1024,1024]{2,1,0:T(8,128)(2,1)} %param.11) | copy-start | bytes 6291460
  4.0 11.7 %slice-start.7 = ((s8[10485760]{0:T(1024)(128)(4,1)}), s8[4194304]{0:T(1024)(128)(4,1)S(1)}, s32[]{:S(2)}) async-start(s8[10485760]{0:T(1024)(128)(4,1)} %bitcast.117), calls=%async_computation.7 | async-start | bytes 8388608
  4.1 11.7 %slice-start.8 = ((s8[10485760]{0:T(1024)(128)(4,1)}), s8[2097152]{0:T(1024)(128)(4,1)S(1)}, s32[]{:S(2)}) async-start(s8[10485760]{0:T(1024)(128)(4,1)} %bitcast.117), calls=%async_computation.8 | async-start | bytes 4194304
  28.0 21.1 %slice-start = ((s8[10485760]{0:T(1024)(128)(4,1)}), s8[2097152]{0:T(1024)(128)(4,1)S(1)}, s32[]{:S(2)}) async-start(s8[10485760]{0:T(1024)(128)(4,1)} %bitcast.113), calls=%async_computation | async-start | bytes 4194304
  28.0 21.1 %slice-start.1 = ((s8[10485760]{0:T(1024)(128)(4,1)}), s8[4194304]{0:T(1024)(128)(4,1)S(1)}, s32[]{:S(2)}) async-start(s8[10485760]{0:T(1024)(128)(4,1)} %bitcast.113), calls=%async_computation.1 | async-start | bytes 8388608
  37.5 76.1 %copy-start.2 = (bf16[1024,1024]{0,1:T(8,128)(2,1)}, bf16[1024,1024]{0,1:T(8,128)(2,1)S(1)}, u32[]{:S(2)}) copy-start(bf16[1024,1024]{0,1:T(8,128)(2,1)S(1)} %get-tuple-element.39) | copy-start | bytes 6291460
  37.5 11.6 %slice-start.2 = ((s8[10485760]{0:T(1024)(128)(4,1)}), s8[4194304]{0:T(1024)(128)(4,1)S(1)}, s32[]{:S(2)}) async-start(s8[10485760]{0:T(1024)(128)(4,1)} %bitcast.113), calls=%async_computation.2 | async-start | bytes 8388608
  37.5 11.6 %copy-start.4 = (bf16[1,1024,1024]{2,1,0:T(8,128)(2,1)S(1)}, bf16[1,1024,1024]{2,1,0:T(8,128)(2,1)}, u32[]{:S(2)}) copy-start(bf16[1,1024,1024]{2,1,0:T(8,128)(2,1)} %param.12) | copy-start | bytes 6291460
  84.8 7.3 %copy-start.7 = (bf16[1024,2560]{1,0:T(8,128)(2,1)S(1)}, bf16[1024,2560]{1,0:T(8,128)(2,1)}, u32[]{:S(2)}) copy-start(bf16[1024,2560]{1,0:T(8,128)(2,1)} %convolution_convert_fusion.3) | copy-start | bytes 15728644
  126.1 14.3 %slice-start.3 = ((s8[10485760]{0:T(1024)(128)(4,1)}), s8[4194304]{0:T(1024)(128)(4,1)S(1)}, s32[]{:S(2)}) async-start(s8[10485760]{0:T(1024)(128)(4,1)} %bitcast.115), calls=%async_computation.3 | async-start | bytes 8388608
  130.0 10.3 %slice-start.4 = ((s8[10485760]{0:T(1024)(128)(4,1)}), s8[4194304]{0:T(1024)(128)(4,1)S(1)}, s32[]{:S(2)}) async-start(s8[10485760]{0:T(1024)(128)(4,1)} %bitcast.115), calls=%async_computation.4 | async-start | bytes 8388608
  130.0 10.3 %slice-start.5 = ((s8[10485760]{0:T(1024)(128)(4,1)}), s8[2097152]{0:T(1024)(128)(4,1)S(1)}, s32[]{:S(2)}) async-start(s8[10485760]{0:T(1024)(128)(4,1)} %bitcast.115), calls=%async_computation.5 | async-start | bytes 4194304
  140.4 5.9 %copy-start.1 = (bf16[1,1024,1024]{1,2,0:T(8,128)(2,1)S(1)}, bf16[1,1024,1024]{1,2,0:T(8,128)(2,1)}, u32[]{:S(2)}) copy-start(bf16[1,1024,1024]{1,2,0:T(8,128)(2,1)} %copy-done) | copy-start | bytes 6291460
  140.4 5.9 %copy-start.6 = (f32[1024]{0:T(1024)S(1)}, f32[1024]{0:T(1024)}, u32[]{:S(2)}) copy-start(f32[1024]{0:T(1024)} %copy-done.5) | copy-start | bytes 12292
